TPU v7x, 16 devices: a 4x2x1 block of a 4x4x8 slice. The times are simulated.
16 devices in a mesh: rep: 2 (over y, z), dp: 8 (over x, core).
Axes of the slice: x: 4, y: 2, z: 1, core: 2. Of those that a mesh axis runs over, the one named last changes fastest.
The devices are a block of a 4x4x8 slice.
Arguments:
- x: bfloat16 [16, 2048, 1280], P(('rep', 'dp')), parts along dimension 0
- dy: bfloat16 [16, 2048, 1280], P(('rep', 'dp')), parts along dimension 0
- w_gate: bfloat16 [2, 1280, 4480], P(None, 'dp')
- w_up: bfloat16 [2, 1280, 4480], P(None, 'dp')
- w_down: bfloat16 [2, 4480, 1280], P(None, 'dp')
- m_w_gate: float32 [2, 1280, 4480], P(None, 'dp')
- m_w_up: float32 [2, 1280, 4480], P(None, 'dp')
- m_w_down: float32 [2, 4480, 1280], P(None, 'dp')
- v_w_gate: float32 [2, 1280, 4480], P(None, 'dp')
- v_w_up: float32 [2, 1280, 4480], P(None, 'dp')
- v_w_down: float32 [2, 4480, 1280], P(None, 'dp')
Outputs:
- output 1: bfloat16 [4, 1280, 4480], P('rep', 'dp'), parts along dimension 0
- output 2: bfloat16 [4, 1280, 4480], P('rep', 'dp'), parts along dimension 0
- output 3: bfloat16 [4, 4480, 1280], P('rep', 'dp'), parts along dimension 0
- output 4: float32 [4, 1280, 4480], P('rep', 'dp'), parts along dimension 0
- output 5: float32 [4, 1280, 4480], P('rep', 'dp'), parts along dimension 0
- output 6: float32 [4, 4480, 1280], P('rep', 'dp'), parts along dimension 0
- output 7: float32 [4, 1280, 4480], P('rep', 'dp'), parts along dimension 0
- output 8: float32 [4, 1280, 4480], P('rep', 'dp'), parts along dimension 0
- output 9: float32 [4, 4480, 1280], P('rep', 'dp'), parts along dimension 0
There are 2 independent parts. A program takes and returns all parts, laid end to end along the dimension named above; an argument that names none is the same for every part.
All inputs are finite; a program needn't handle non-finite values.
Results may differ from a plain program's by a relative error of at most 0.022.
Values are sent between devices in bfloat16 or wider.
A program may use at most 768 MiB of HBM per device.

v0:
```python
import jax
import jax.numpy as jnp
from jax import lax
from jax.sharding import PartitionSpec as P

NAMES = ("w_gate", "w_up", "w_down")


def matmul(a, w):
    return jnp.dot(a, w, preferred_element_type=jnp.float32).astype(jnp.bfloat16)


def normed(h):
    wide = h.astype(jnp.float32)
    scale = lax.rsqrt(jnp.mean(wide**2, -1, keepdims=True) + 1e-6)
    return (wide * scale).astype(jnp.bfloat16)


def layer(h, w):
    a = normed(h)
    gate = jnp.dot(a, w["w_gate"], preferred_element_type=jnp.float32)
    up = jnp.dot(a, w["w_up"], preferred_element_type=jnp.float32)
    return h + matmul((jax.nn.silu(gate) * up).astype(jnp.bfloat16), w["w_down"])


def adamw(w, m, v, g):
    m = 0.9 * m + 0.1 * g
    v = 0.95 * v + 0.05 * g * g
    step = m * lax.rsqrt(v + 1e-8) + 0.1 * w
    return (w - 0.02 * step).astype(jnp.bfloat16), m, v


def clipped(gradients, sum_of_squares, count):
    factor = jnp.minimum(1.0, 0.5 * lax.rsqrt(sum_of_squares / count + 1e-30))
    return [g * factor for g in gradients]


def solution(mesh):
    def fetched(weights, number):
        return {name: lax.all_gather(w[number], "dp", axis=0, tiled=True) for name, w in zip(NAMES, weights, strict=True)}

    def step(x, dy, *arrays):
        weights, m, v = (arrays[i : i + 3] for i in (0, 3, 6))
        layers = weights[0].shape[0]
        h, kept = x[0], []
        for number in range(layers):
            kept.append(h)
            h = layer(h, fetched(weights, number))
        by_h, mine = dy[0], [None] * layers
        for number in reversed(range(layers)):
            _, back = jax.vjp(lambda w, h: layer(h, w), fetched(weights, number), kept[number])
            by_w, by_h = back(by_h)
            mine[number] = [lax.psum_scatter(by_w[name], "dp", scatter_dimension=0, tiled=True) for name in NAMES]
        gradients = [jnp.stack([mine[number][i] for number in range(layers)]).astype(jnp.float32) for i in range(3)]
        squares = lax.psum(sum(jnp.sum(g * g) for g in gradients), "dp")
        gradients = clipped(gradients, squares, lax.psum(1, "dp") * sum(g.size for g in gradients))
        new = [adamw(w.astype(jnp.float32), m, v, g) for w, m, v, g in zip(weights, m, v, gradients, strict=True)]
        return tuple(one[which] for which in range(3) for one in new)

    states, cut = P(("rep", "dp"), None, None), P(None, "dp", None)
    return jax.shard_map(
        step,
        mesh=mesh,
        in_specs=(states, states) + (cut,) * 9,
        out_specs=(P("rep", "dp", None),) * 9,
        check_vma=False,
    )
```

profile of v0, /device:TPU:113, one launch (start us, length us, event | category | flops | bytes accessed | tf_op | source)
XLA Modules:
  0.0 990.8 jit_solution(12830707241988385355)
XLA Ops:
  7.2 0.1 all-gather.13.cloned.1.call-start
  7.3 3.6 fusion.103
  10.8 0.1 all-gather.13.cloned.1.call-update
  10.9 0.1 all-gather.15.cloned.1.call-start
  10.9 3.7 fusion.102
  14.7 0.1 all-gather.15.cloned.1.call-update
  14.7 0.1 all-gather.17.cloned.1.call-start
  14.8 1.8 fusion.101
  16.6 0.1 all-gather.17.cloned.1.call-update
  16.6 0.1 all-gather.21.cloned.1.call-start
  16.7 0.6 all-gather.21.cloned.1.call-update
  17.3 0.1 all-gather.23.cloned.1.call-start
  17.3 0.6 all-gather.23.cloned.1.call-update
  17.9 0.1 all-gather.19.cloned.1.call-start
  18.0 0.6 all-gather.19.cloned.1.call-update
  18.5 0.1 reduce-scatter.15.cloned.1.call-start
  18.6 7.9 copy.20
  26.5 3.6 fusion.34
  30.1 7.9 copy.21
  38.0 34.9 %all-gather.13.cloned.1.call-done = bf16[1,1280,4480]{2,1,0:T(8,128)(2,1)} async-done(((bf16[1,160,4480]{2,1,0:T(8,128)(2,1)}), bf16[1,1280,4480]{2,1,0:T(8,128)(2,1)}) %all-gather.13.cloned.1.call-update) | async-done | bytes 11468816 | tf_op jit(solution)/shard_map/all_gather | solution.py:40
  72.9 32.1 %fusion.32 = f32[2048,4480]{1,0:T(8,128)} fusion(bf16[1,1280,4480]{2,1,0:T(8,128)(2,1)} %all-gather.13.cloned.1.call-done, bf16[1,2048,1280]{1,2,0:T(8,128)(2,1)} %copy.20, f32[2048]{0:T(1024)S(1)} %add_rsqrt_fusion), kind=kOutput, calls=%fused_computation.51 | convolution fusion | flops 23495966720 | bytes 53420032 | tf_op jit(solution)/shard_map/dot_general | solution.py:21
  104.9 29.0 %all-gather.15.cloned.1.call-done = bf16[1,1280,4480]{2,1,0:T(8,128)(2,1)} async-done(((bf16[1,160,4480]{2,1,0:T(8,128)(2,1)}), bf16[1,1280,4480]{2,1,0:T(8,128)(2,1)}) %all-gather.15.cloned.1.call-update) | async-done | bytes 11468816 | tf_op jit(solution)/shard_map/all_gather | solution.py:40
  133.9 45.2 %multiply_convert_fusion.1 = (bf16[2048,4480]{1,0:T(8,128)(2,1)}, f32[2048,4480]{1,0:T(8,128)}) fusion(f32[2048,4480]{1,0:T(8,128)} %fusion.32, bf16[1,1280,4480]{2,1,0:T(8,128)(2,1)} %all-gather.15.cloned.1.call-done, bf16[1,2048,1280]{1,2,0:T(8,128)(2,1)} %copy.20, f32[2048]{0:T(1024)S(1)} %add_rsqrt_fusion), kind=kOutput, calls=%fused_computation.17 | convolution fusion | flops 23551016960 | bytes 108470272 | tf_op jit(solution)/shard_map/dot_general | solution.py:22
  179.1 15.8 %all-gather.17.cloned.1.call-done = bf16[1,4480,1280]{2,1,0:T(8,128)(2,1)} async-done(((bf16[1,560,1280]{2,1,0:T(8,128)(2,1)}), bf16[1,4480,1280]{2,1,0:T(8,128)(2,1)}) %all-gather.17.cloned.1.call-update) | async-done | bytes 11468816 | tf_op jit(solution)/shard_map/all_gather | solution.py:40
  194.9 33.0 %fusion.38 = (f32[2048]{0:T(1024)S(1)}, bf16[2048,1280]{0,1:T(8,128)(2,1)}) fusion(bf16[2048,4480]{1,0:T(8,128)(2,1)} %get-tuple-element.24, bf16[1,4480,1280]{2,1,0:T(8,128)(2,1)} %all-gather.17.cloned.1.call-done, bf16[1,2048,1280]{1,2,0:T(8,128)(2,1)} %copy.20), kind=kOutput, calls=%fused_computation.57 | convolution fusion | flops 23501207552 | bytes 40312832 | tf_op jit(solution)/shard_map/dot_general | solution.py:10
  228.0 27.9 %all-gather.21.cloned.1.call-done = bf16[1,4480,1280]{2,1,0:T(8,128)(2,1)} async-done(((bf16[1,560,1280]{2,1,0:T(8,128)(2,1)}), bf16[1,4480,1280]{2,1,0:T(8,128)(2,1)}) %all-gather.21.cloned.1.call-update) | async-done | bytes 11468816 | tf_op jit(solution)/shard_map/all_gather | solution.py:40
  255.8 31.7 %convolution_convert_fusion.1 = bf16[2048,4480]{1,0:T(8,128)(2,1)} fusion(bf16[1,4480,1280]{2,1,0:T(8,128)(2,1)} %all-gather.21.cloned.1.call-done, bf16[1,2048,1280]{2,1,0:T(8,128)(2,1)} %param.12), kind=kOutput, calls=%fused_computation.26 | convolution fusion | flops 23497277440 | bytes 35061760 | tf_op jit(solution)/shard_map/transpose(jvp())/dot_general | solution.py:10
  287.5 29.2 %all-gather.23.cloned.1.call-done = bf16[1,1280,4480]{2,1,0:T(8,128)(2,1)} async-done(((bf16[1,160,4480]{2,1,0:T(8,128)(2,1)}), bf16[1,1280,4480]{2,1,0:T(8,128)(2,1)}) %all-gather.23.cloned.1.call-update) | async-done | bytes 11468816 | tf_op jit(solution)/shard_map/all_gather | solution.py:40
  316.7 32.1 %fusion.19 = f32[2048,4480]{1,0:T(8,128)} fusion(bf16[1,1280,4480]{2,1,0:T(8,128)(2,1)} %all-gather.23.cloned.1.call-done, bf16[2048,1280]{0,1:T(8,128)(2,1)} %get-tuple-element.27, f32[2048]{0:T(1024)S(1)} %fusion.89), kind=kOutput, calls=%fused_computation.38 | convolution fusion | flops 23495966720 | bytes 53420032 | tf_op jit(solution)/shard_map/jvp()/dot_general | solution.py:22
  348.8 28.8 %all-gather.19.cloned.1.call-done = bf16[1,1280,4480]{2,1,0:T(8,128)(2,1)} async-done(((bf16[1,160,4480]{2,1,0:T(8,128)(2,1)}), bf16[1,1280,4480]{2,1,0:T(8,128)(2,1)}) %all-gather.19.cloned.1.call-update) | async-done | bytes 11468816 | tf_op jit(solution)/shard_map/all_gather | solution.py:40
  377.6 54.4 %fusion.2 = (bf16[2048,4480]{1,0:T(8,128)(2,1)}, f32[2048,4480]{1,0:T(8,128)}) fusion(f32[2048,4480]{1,0:T(8,128)} %fusion.19, bf16[2048,4480]{1,0:T(8,128)(2,1)} %convolution_convert_fusion.1, bf16[1,1280,4480]{2,1,0:T(8,128)(2,1)} %all-gather.19.cloned.1.call-done, bf16[2048,1280]{0,1:T(8,128)(2,1)} %get-tuple-element.27, f32[2048]{0:T(1024)S(1)} %fusion.89), kind=kOutput, calls=%fused_computation.8 | convolution fusion | flops 23606067200 | bytes 126820352 | tf_op jit(solution)/shard_map/jvp()/dot_general | solution.py:21
  432.0 35.2 %fusion.44 = bf16[2048,1280]{0,1:T(8,128)(2,1)} fusion(bf16[1,1280,4480]{2,1,0:T(8,128)(2,1)} %all-gather.23.cloned.1.call-done, bf16[2048,4480]{1,0:T(8,128)(2,1)} %convolution_convert_fusion.1, f32[2048,4480]{1,0:T(8,128)} %get-tuple-element.29), kind=kOutput, calls=%fused_computation.64 | convolution fusion | flops 23545774080 | bytes 71761920 | tf_op jit(solution)/shard_map/transpose(jvp())/dot_general | solution.py:22
  467.2 34.2 %fusion.40 = (f32[2048]{0:T(1024)S(1)}, bf16[2048,1280]{0,1:T(8,128)(2,1)}) fusion(bf16[2048,1280]{0,1:T(8,128)(2,1)} %get-tuple-element.27, bf16[2048,1280]{0,1:T(8,128)(2,1)} %fusion.44, bf16[2048,4480]{1,0:T(8,128)(2,1)} %get-tuple-element.28, bf16[1,1280,4480]{2,1,0:T(8,128)(2,1)} %all-gather.19.cloned.1.call-done), kind=kOutput, calls=%fused_computation.59 | convolution fusion | flops 23501207552 | bytes 45555712 | tf_op jit(solution)/shard_map/transpose(jvp())/dot_general | solution.py:21
  501.4 12.4 %fusion.78 = bf16[2048,1280]{0,1:T(8,128)(2,1)} fusion(bf16[2048,1280]{0,1:T(8,128)(2,1)} %get-tuple-element.27, bf16[2048,1280]{0,1:T(8,128)(2,1)} %get-tuple-element.31, bf16[1,2048,1280]{1,2,0:T(8,128)(2,1)} %copy.21, f32[2048]{0:T(1024)S(1)} %multiply_multiply_fusion.3, f32[2048]{0:T(1024)S(1)} %fusion.89), kind=kLoop, calls=%fused_computation.101 | loop fusion | flops 18350080 | bytes 20987904 | tf_op jit(solution)/shard_map/transpose(jvp())/add_any | solution.py:14
  513.8 29.8 %convolution_convert_fusion.3 = bf16[4480,1280]{1,0:T(8,128)(2,1)} fusion(bf16[2048,4480]{1,0:T(8,128)(2,1)} %get-tuple-element.24, bf16[2048,1280]{0,1:T(8,128)(2,1)} %fusion.78), kind=kOutput, calls=%fused_computation.28 | convolution fusion | flops 23493836800 | bytes 35061760 | tf_op jit(solution)/shard_map/transpose(jvp())/dot_general | solution.py:10
  543.6 0.1 reduce-scatter.15.cloned.1.call-update
  543.7 0.1 reduce-scatter.17.cloned.1.call-start
  543.8 38.7 %convolution_convert_fusion.2 = bf16[4480,1280]{1,0:T(8,128)(2,1)} fusion(f32[2048,4480]{1,0:T(8,128)} %fusion.19, bf16[1,2048,1280]{2,1,0:T(8,128)(2,1)} %param.12, f32[2048,4480]{1,0:T(8,128)} %get-tuple-element.29), kind=kOutput, calls=%fused_computation.27 | convolution fusion | flops 23548887040 | bytes 90112000 | tf_op jit(solution)/shard_map/transpose(jvp())/dot_general | solution.py:10
  582.5 0.1 reduce-scatter.17.cloned.1.call-update
  582.5 0.1 reduce-scatter.11.cloned.1.call-start
  582.6 32.0 %convolution_convert_fusion = bf16[2048,4480]{1,0:T(8,128)(2,1)} fusion(bf16[2048,1280]{0,1:T(8,128)(2,1)} %fusion.78, bf16[1,4480,1280]{2,1,0:T(8,128)(2,1)} %all-gather.17.cloned.1.call-done), kind=kOutput, calls=%fused_computation.25 | convolution fusion | flops 23497277440 | bytes 35061760 | tf_op jit(solution)/shard_map/transpose(jvp())/dot_general | solution.py:10
  614.6 37.6 %fusion.17 = bf16[1280,4480]{1,0:T(8,128)(2,1)} fusion(bf16[2048,4480]{1,0:T(8,128)(2,1)} %convolution_convert_fusion, f32[2048,4480]{1,0:T(8,128)} %fusion.32, bf16[1,2048,1280]{1,2,0:T(8,128)(2,1)} %copy.20, f32[2048]{0:T(1024)S(1)} %copy-done.13), kind=kOutput, calls=%fused_computation.24 | convolution fusion | flops 23556751360 | bytes 71770112 | tf_op jit(solution)/shard_map/transpose(jvp())/dot_general | solution.py:22
  652.2 0.1 reduce-scatter.11.cloned.1.call-update
  652.3 0.1 reduce-scatter.13.cloned.1.call-start
  652.3 0.6 copy-done.9
  652.9 37.5 %fusion.13 = bf16[1280,4480]{1,0:T(8,128)(2,1)} fusion(bf16[2048,4480]{1,0:T(8,128)(2,1)} %convolution_convert_fusion.1, bf16[2048,1280]{0,1:T(8,128)(2,1)} %get-tuple-element.27, f32[2048]{0:T(1024)S(1)} %copy-done.9, f32[2048,4480]{1,0:T(8,128)} %get-tuple-element.29), kind=kOutput, calls=%fused_computation.22 | convolution fusion | flops 23556751360 | bytes 71770112 | tf_op jit(solution)/shard_map/transpose(jvp())/dot_general | solution.py:22
  690.4 0.1 reduce-scatter.13.cloned.1.call-update
  690.5 0.1 reduce-scatter.7.cloned.1.call-start
  690.6 44.7 %fusion.14 = bf16[1280,4480]{1,0:T(8,128)(2,1)} fusion(f32[2048,4480]{1,0:T(8,128)} %fusion.32, f32[2048,4480]{1,0:T(8,128)} %get-tuple-element.25, bf16[2048,4480]{1,0:T(8,128)(2,1)} %convolution_convert_fusion, bf16[1,2048,1280]{1,2,0:T(8,128)(2,1)} %copy.20, f32[2048]{0:T(1024)S(1)} %copy-done.13), kind=kOutput, calls=%fused_computation.23 | convolution fusion | flops 23602626560 | bytes 108470272 | tf_op jit(solution)/shard_map/transpose(jvp())/dot_general | solution.py:21
  735.3 0.1 reduce-scatter.7.cloned.1.call-update
  735.4 0.1 reduce-scatter.9.cloned.1.call-start
  735.4 31.5 %convolution_convert_fusion.4 = bf16[1280,4480]{1,0:T(8,128)(2,1)} fusion(bf16[2048,4480]{1,0:T(8,128)(2,1)} %get-tuple-element.28, bf16[2048,1280]{0,1:T(8,128)(2,1)} %get-tuple-element.27, f32[2048]{0:T(1024)S(1)} %copy-done.9), kind=kOutput, calls=%fused_computation.29 | convolution fusion | flops 23495966720 | bytes 35069952 | tf_op jit(solution)/shard_map/transpose(jvp())/dot_general | solution.py:21
  767.0 0.1 reduce-scatter.9.cloned.1.call-update
  767.1 4.0 fusion.68
  771.1 30.5 %reduce-scatter.13.cloned.1.call-done = bf16[160,4480]{1,0:T(8,128)(2,1)} async-done(((bf16[1280,4480]{1,0:T(8,128)(2,1)}), bf16[160,4480]{1,0:T(8,128)(2,1)}) %reduce-scatter.13.cloned.1.call-update) | async-done | bytes 1433616 | tf_op jit(solution)/shard_map/reduce_scatter | solution.py:53
  801.6 3.9 fusion.67
  805.5 61.2 %reduce-scatter.7.cloned.1.call-done = bf16[160,4480]{1,0:T(8,128)(2,1)} async-done(((bf16[1280,4480]{1,0:T(8,128)(2,1)}), bf16[160,4480]{1,0:T(8,128)(2,1)}) %reduce-scatter.7.cloned.1.call-update) | async-done | bytes 1433616 | tf_op jit(solution)/shard_map/reduce_scatter | solution.py:53
  866.7 65.0 %reduce-scatter.9.cloned.1.call-done = bf16[160,4480]{1,0:T(8,128)(2,1)} async-done(((bf16[1280,4480]{1,0:T(8,128)(2,1)}), bf16[160,4480]{1,0:T(8,128)(2,1)}) %reduce-scatter.9.cloned.1.call-update) | async-done | bytes 1433616 | tf_op jit(solution)/shard_map/reduce_scatter | solution.py:53
  931.7 3.9 fusion.66
  937.5 13.8 %psum.7 = f32[]{:T(128)} all-reduce(f32[]{:T(128)S(6)} %add.99), channel_id=1, replica_groups=mesh['rep'=2,'dp'=8] {'dp'}, use_global_device_ids=true, to_apply=%region_12.13 | all-reduce | flops 1 | bytes 8 | tf_op jit(solution)/shard_map/psum | solution.py:55
  952.0 11.9 %fusion.74 = (bf16[2,560,1280]{2,1,0:T(8,128)(2,1)}, f32[2,560,1280]{2,1,0:T(8,128)}, f32[2,560,1280]{2,1,0:T(8,128)}) fusion(bf16[2,560,1280]{2,1,0:T(8,128)(2,1)S(1)} %copy-done.1, f32[]{:T(128)S(6)} %min_shard_map.3, bf16[1,560,1280]{2,1,0:T(8,128)(2,1)} %bitcast.78, bf16[1,560,1280]{2,1,0:T(8,128)(2,1)} %bitcast.76, f32[2,560,1280]{2,1,0:T(8,128)} %param.21, ...), kind=kLoop, calls=%fused_computation.97 | loop fusion | flops 28672000 | bytes 31539204 | tf_op jit(solution)/shard_map/convert_element_type | solution.py:30
  964.0 0.9 copy-done.6
  964.9 0.4 copy-done.7
  965.3 18.1 %fusion.65 = (bf16[2,160,4480]{2,1,0:T(8,128)(2,1)}, f32[2,160,4480]{2,1,0:T(8,128)}, f32[2,160,4480]{2,1,0:T(8,128)}, bf16[2,160,4480]{2,1,0:T(8,128)(2,1)}, f3...) fusion(bf16[2,160,4480]{2,1,0:T(8,128)(2,1)S(1)} %copy-done.2, f32[]{:T(128)S(6)} %min_shard_map.3, ...), kind=kLoop, calls=%fused_computation.88 | loop fusion | flops 57344000 | bytes 63078404 | tf_op jit(solution)/shard_map/convert_element_type | solution.py:30
  (31 shorter events, 0.1 us)
Async XLA Ops:
  7.2 65.7 %all-gather.13.cloned.1.call-start = ((), (), s32[]{:S(2)}) async-start(), calls=%async_computation.12 | async-start | bytes 12902400 | tf_op jit(solution)/shard_map/all_gather | solution.py:40
  10.8 4.0 copy-start
  10.9 123.0 %all-gather.15.cloned.1.call-start = ((), (), s32[]{:S(2)}) async-start(), calls=%async_computation.13 | async-start | bytes 12902400 | tf_op jit(solution)/shard_map/all_gather | solution.py:40
  14.7 180.2 %all-gather.17.cloned.1.call-start = ((), (), s32[]{:S(2)}) async-start(), calls=%async_computation.14 | async-start | bytes 12902400 | tf_op jit(solution)/shard_map/all_gather | solution.py:40
  16.6 239.2 %all-gather.21.cloned.1.call-start = ((), (), s32[]{:S(2)}) async-start(), calls=%async_computation.16 | async-start | bytes 12902400 | tf_op jit(solution)/shard_map/all_gather | solution.py:40
  17.3 299.5 %all-gather.23.cloned.1.call-start = ((), (), s32[]{:S(2)}) async-start(), calls=%async_computation.17 | async-start | bytes 12902400 | tf_op jit(solution)/shard_map/all_gather | solution.py:40
  17.9 359.7 %all-gather.19.cloned.1.call-start = ((), (), s32[]{:S(2)}) async-start(), calls=%async_computation.15 | async-start | bytes 12902400 | tf_op jit(solution)/shard_map/all_gather | solution.py:40
  18.5 748.5 %reduce-scatter.15.cloned.1.call-start = ((), (), s32[]{:S(2)}) async-start(), calls=%async_computation.10 | async-start | bytes 12902400 | tf_op jit(solution)/shard_map/reduce_scatter | solution.py:53
  30.1 103.8 %copy-start.12 = (f32[2048]{0:T(1024)}, f32[2048]{0:T(1024)S(1)}, u32[]{:S(2)}) copy-start(f32[2048]{0:T(1024)S(1)} %add_rsqrt_fusion) | copy-start | bytes 24580
  227.9 59.6 %copy-start.10 = (f32[2048]{0:T(1024)}, f32[2048]{0:T(1024)S(1)}, u32[]{:S(2)}) copy-start(f32[2048]{0:T(1024)S(1)} %get-tuple-element.26) | copy-start | bytes 24580
  227.9 273.5 %copy-start.8 = (f32[2048]{0:T(1024)}, f32[2048]{0:T(1024)S(1)}, u32[]{:S(2)}) copy-start(f32[2048]{0:T(1024)S(1)} %fusion.89) | copy-start | bytes 24580
  467.2 34.2 %copy-start.11 = (f32[2048]{0:T(1024)S(1)}, f32[2048]{0:T(1024)}, u32[]{:S(2)}) copy-start(f32[2048]{0:T(1024)} %copy-done.10) | copy-start | bytes 24580
  543.7 223.4 %reduce-scatter.17.cloned.1.call-start = ((), (), s32[]{:S(2)}) async-start(), calls=%async_computation.11 | async-start | bytes 12902400 | tf_op jit(solution)/shard_map/reduce_scatter | solution.py:53
  582.5 32.1 %copy-start.13 = (f32[2048]{0:T(1024)S(1)}, f32[2048]{0:T(1024)}, u32[]{:S(2)}) copy-start(f32[2048]{0:T(1024)} %copy-done.12) | copy-start | bytes 24580
  582.5 188.6 %reduce-scatter.11.cloned.1.call-start = ((), (), s32[]{:S(2)}) async-start(), calls=%async_computation.8 | async-start | bytes 12902400 | tf_op jit(solution)/shard_map/reduce_scatter | solution.py:53
  652.2 0.7 copy-start.9
  652.3 149.3 %reduce-scatter.13.cloned.1.call-start = ((), (), s32[]{:S(2)}) async-start(), calls=%async_computation.9 | async-start | bytes 12902400 | tf_op jit(solution)/shard_map/reduce_scatter | solution.py:53
  690.5 176.2 %reduce-scatter.7.cloned.1.call-start = ((), (), s32[]{:S(2)}) async-start(), calls=%async_computation.6 | async-start | bytes 12902400 | tf_op jit(solution)/shard_map/reduce_scatter | solution.py:53
  735.4 196.3 %reduce-scatter.9.cloned.1.call-start = ((), (), s32[]{:S(2)}) async-start(), calls=%async_computation.7 | async-start | bytes 12902400 | tf_op jit(solution)/shard_map/reduce_scatter | solution.py:53
  767.0 184.9 %copy-start.1 = (bf16[2,560,1280]{2,1,0:T(8,128)(2,1)S(1)}, bf16[2,560,1280]{2,1,0:T(8,128)(2,1)}, u32[]{:S(2)}) copy-start(bf16[2,560,1280]{2,1,0:T(8,128)(2,1)} %param.15) | copy-start | bytes 8601604
  951.9 12.0 %copy-start.2 = (bf16[2,160,4480]{2,1,0:T(8,128)(2,1)S(1)}, bf16[2,160,4480]{2,1,0:T(8,128)(2,1)}, u32[]{:S(2)}) copy-start(bf16[2,160,4480]{2,1,0:T(8,128)(2,1)} %param.13) | copy-start | bytes 8601604
  952.0 12.0 %copy-start.3 = (bf16[2,160,4480]{2,1,0:T(8,128)(2,1)S(1)}, bf16[2,160,4480]{2,1,0:T(8,128)(2,1)}, u32[]{:S(2)}) copy-start(bf16[2,160,4480]{2,1,0:T(8,128)(2,1)} %param.14) | copy-start | bytes 8601604
  952.0 12.0 %copy-start.4 = (bf16[160,4480]{1,0:T(8,128)(2,1)S(1)}, bf16[160,4480]{1,0:T(8,128)(2,1)}, u32[]{:S(2)}) copy-start(bf16[160,4480]{1,0:T(8,128)(2,1)} %reduce-scatter.11.cloned.1.call-done) | copy-start | bytes 4300804
  952.0 12.0 %copy-start.5 = (bf16[160,4480]{1,0:T(8,128)(2,1)S(1)}, bf16[160,4480]{1,0:T(8,128)(2,1)}, u32[]{:S(2)}) copy-start(bf16[160,4480]{1,0:T(8,128)(2,1)} %reduce-scatter.13.cloned.1.call-done) | copy-start | bytes 4300804
  952.0 12.9 %copy-start.6 = (bf16[160,4480]{1,0:T(8,128)(2,1)S(1)}, bf16[160,4480]{1,0:T(8,128)(2,1)}, u32[]{:S(2)}) copy-start(bf16[160,4480]{1,0:T(8,128)(2,1)} %reduce-scatter.7.cloned.1.call-done) | copy-start | bytes 4300804
  952.0 13.3 %copy-start.7 = (bf16[160,4480]{1,0:T(8,128)(2,1)S(1)}, bf16[160,4480]{1,0:T(8,128)(2,1)}, u32[]{:S(2)}) copy-start(bf16[160,4480]{1,0:T(8,128)(2,1)} %reduce-scatter.9.cloned.1.call-done) | copy-start | bytes 4300804
Sparse Core Ops, SparseCore 0:
  11.0 61.8 all-gather.12
  75.0 58.8 all-gather.14
  136.1 58.8 all-gather.16
  197.0 58.8 all-gather.20
  257.8 58.8 all-gather.22
  318.7 58.8 all-gather.18
  543.8 62.5 reduce-scatter.14
  608.8 62.7 reduce-scatter.16
  673.8 62.7 reduce-scatter.10
  738.8 62.7 reduce-scatter.12
  803.9 62.7 reduce-scatter.6
  868.9 62.7 reduce-scatter.8
where the time goes:
time: 997 us; the launch traced here: 991 us
  matrix products  550 us (55%)
  waiting for transfers between devices  325 us (33%)
  other arithmetic  57.8 us (6%)
  local copies, waits for them, and re-layouts  26.8 us (3%)
  between operations  17.6 us (2%)
  blocking collectives  13.8 us (1%)
    dot_general x5, matrix products, layer(): gate = jnp.dot(a, w['w_gate'], preferred_element_type=jnp.float32)  197 us
    dot_general x5, matrix products, layer(): up = jnp.dot(a, w['w_up'], preferred_element_type=jnp.float32)  188 us
    all_gather x6, waiting for transfers between devices, fetched(): lax.all_gather(w[number], 'dp', axis=0, tiled=True)  166 us
    dot_general x5, matrix products, matmul(): jnp.dot(a, w, preferred_element_type=jnp.float32).astype(jnp.bfloat16)  165 us
    reduce_scatter x6, waiting for transfers between devices, step(): lax.psum_scatter(by_w[name], 'dp', scatter_dimension=0, tiled=True)  157 us
    convert_element_type x2, other arithmetic, adamw(): return ((w - 0.02 * step).astype(jnp.bfloat16), m, v)  30 us
  transfers between devices with their start and end apart: 12, of which 9 were waited for; matrix products, arithmetic and copies ran while one was open for 43% of the time, Pallas kernels for 0%

commit v1 on v0

v1 whole, which is shorter than its diff:
```python
import functools

import jax
import jax.numpy as jnp
from jax import lax
from jax.experimental import pallas as pl
from jax.experimental.pallas import tpu as pltpu
from jax.sharding import PartitionSpec as P

BF = jnp.bfloat16
WIDE, DEEP = 640, 256


def dot(a, b, dims):
    return lax.dot_general(a, b, (dims, ((), ())), preferred_element_type=jnp.float32)


def adamw(w, m, v, g):
    m = 0.9 * m + 0.1 * g
    v = 0.95 * v + 0.05 * g * g
    step = m * lax.rsqrt(v + 1e-8) + 0.1 * w
    return (w - 0.02 * step).astype(BF), m, v


MESH = pl.DeviceIdType.MESH
SECOND, THIRD, FOURTH, READY = 1, 2, 3, 4


def pieces(rows):
    theirs = rows * 3 // 10 // 16 * 16
    return rows - theirs, theirs


def forward_kernel(n, wide, deep, x_hbm, wg_hbm, wu_hbm, wd_hbm, g_hbm, u_hbm, ht_hbm, at_hbm, h_hbm, fg_hbm, fu_hbm, fd_hbm,
                   h, a, hid, wgu, wd, g_out, u_out, t_out, a_t, recv, whole, local, sent, load_g, load_u, load_d, out_sem, io_sem):
    layers, ff = wg_hbm.shape[0], wg_hbm.shape[2]
    tokens, d = x_hbm.shape
    chips, half = n // 2, tokens // 2
    step = half // 4
    ups, downs = ff // wide, d // deep
    per = 2 * ups + downs
    units = layers * per
    rep, me = lax.axis_index("rep"), lax.axis_index("dp")
    chip, core = me // 2, me % 2
    parity = rep % 2
    way = 1 - 2 * core
    there = lambda k: ((chip + k * way + 2 * chips) % chips) * 2 + core
    ahead, behind, across = there(1), there(-1), there(2)
    beside = chip * 2 + 1 - core
    to_ahead, to_behind, to_beside = ((rep, i) for i in (ahead, behind, beside))
    to_pair = (rep + 1 - 2 * parity, me)

    barrier = pltpu.get_barrier_semaphore()
    for device in (to_ahead, to_behind, to_beside, to_pair):
        pl.semaphore_signal(barrier, inc=1, device_id=device, device_id_type=MESH)
    pl.semaphore_wait(barrier, 4)

    def unit_views(kind, layer, chunk):
        block, whole_ref, width = ((wg_hbm, fg_hbm, wide), (wu_hbm, fu_hbm, wide), (wd_hbm, fd_hbm, deep))[kind]
        columns = pl.ds(pl.multiple_of(chunk * width, width), width)
        rows = block.shape[1]
        own = lambda start, size: block.at[layer, pl.ds(pl.multiple_of(start, 16), size), columns]
        full = lambda start, size: whole_ref.at[layer, pl.ds(pl.multiple_of(start, 16), size), columns]
        return rows, own, full

    def for_unit(t, body):
        layer, r = t // per, t % per
        ok = jnp.logical_and(t >= 0, t < units)
        for kind in range(3):
            here = r >= 2 * ups if kind == 2 else jnp.logical_and(r < 2 * ups, r % 2 == kind)

            @pl.when(jnp.logical_and(ok, here))
            def _():
                body(kind, t, layer, r - 2 * ups if kind == 2 else r // 2)

    def send(unit, src, dst, device, sem):
        pltpu.make_async_remote_copy(src_ref=src, dst_ref=dst, send_sem=sent.at[unit], recv_sem=sem, device_id=device, device_id_type=MESH).start()

    def arrived(ref, sem):
        pltpu.make_async_copy(ref, ref, sem).wait()

    def stage_one(kind, unit, layer, chunk):
        rows, own, full = unit_views(kind, layer, chunk)
        mine, theirs = pieces(rows)
        start = parity * theirs
        send(unit, own(start, mine), full(me * rows + start, mine), to_ahead, recv.at[unit, 0])
        send(unit, own(start, mine), full(me * rows + start, mine), to_behind, recv.at[unit, 1])
        send(unit, own(0, rows), full(me * rows, rows), to_beside, whole.at[unit])
        pltpu.make_async_copy(own(0, rows), full(me * rows, rows), local.at[unit]).start()

    def onward(unit, rows, full, block, pair_sem):
        mine, theirs = pieces(rows)
        start, give = block * rows + parity * theirs, block * rows + parity * mine
        send(unit, full(give, theirs), full(give, theirs), to_pair, pair_sem)
        send(unit, full(start, mine), full(start, mine), to_beside, whole.at[unit])

    def from_pair(unit, rows, full, block, sem):
        mine, theirs = pieces(rows)
        ref = full(block * rows + (1 - parity) * mine, theirs)
        arrived(ref, sem)
        send(unit, ref, ref, to_beside, whole.at[unit])

    def stage_two(kind, unit, layer, chunk):
        rows, _, full = unit_views(kind, layer, chunk)
        mine, theirs = pieces(rows)
        first = full(behind * rows + parity * theirs, mine)
        arrived(first, recv.at[unit, 0])
        send(unit, first, first, to_ahead, recv.at[unit, 2])
        onward(unit, rows, full, behind, recv.at[unit, 3])
        arrived(full(ahead * rows + parity * theirs, mine), recv.at[unit, 1])
        onward(unit, rows, full, ahead, recv.at[unit, 4])

    def stage_three(kind, unit, layer, chunk):
        rows, _, full = unit_views(kind, layer, chunk)
        mine, theirs = pieces(rows)
        arrived(full(across * rows + parity * theirs, mine), recv.at[unit, 2])
        onward(unit, rows, full, across, recv.at[unit, 5])
        from_pair(unit, rows, full, behind, recv.at[unit, 3])
        from_pair(unit, rows, full, ahead, recv.at[unit, 4])

    def stage_four(kind, unit, layer, chunk):
        rows, _, full = unit_views(kind, layer, chunk)
        from_pair(unit, rows, full, across, recv.at[unit, 5])

    def ready(kind, unit, layer, chunk):
        rows, own, full = unit_views(kind, layer, chunk)
        arrived(full(0, chips * rows), whole.at[unit])
        arrived(own(0, rows), local.at[unit])
        slot = chunk % 2
        if kind == 0:
            pltpu.make_async_copy(full(0, d), wgu.at[slot, :, pl.ds(0, wide)], load_g.at[slot]).start()
        elif kind == 1:
            pltpu.make_async_copy(full(0, d), wgu.at[slot, :, pl.ds(wide, wide)], load_u.at[slot]).start()
        else:

            @pl.when(layer + 1 < layers)
            def _():
                pltpu.make_async_copy(full(0, ff), wd.at[slot], load_d.at[slot]).start()

    def all_sent(kind, unit, layer, chunk):
        rows, _, full = unit_views(kind, layer, chunk)
        arrived(full(0, (n - 1) * rows), sent.at[unit])

    def norm():
        def some(i, _):
            at = pl.ds(pl.multiple_of(i * 256, 256), 256)
            w = h[at, :].astype(jnp.float32)
            some_a = (w * lax.rsqrt(jnp.mean(w * w, -1, keepdims=True) + 1e-6)).astype(BF)
            a[at, :] = some_a
            a_t[:, at] = some_a.T
            return 0

        lax.fori_loop(0, tokens // 256, some, 0)

    def results(layer, chunk, part):
        at = pl.ds(pl.multiple_of(part * half, half), half)
        columns = pl.ds(pl.multiple_of(chunk * wide, wide), wide)
        return (
            pltpu.make_async_copy(g_out.at[part], g_hbm.at[layer, at, columns], out_sem.at[part, 0]),
            pltpu.make_async_copy(u_out.at[part], u_hbm.at[layer, at, columns], out_sem.at[part, 1]),
            pltpu.make_async_copy(t_out.at[part], ht_hbm.at[layer, columns, at], out_sem.at[part, 2]),
        )

    def gate_up(layer, chunk, part):
        slot = chunk % 2

        @pl.when(part == 0)
        def _():
            arrived(wgu.at[slot, :, pl.ds(0, wide)], load_g.at[slot])
            arrived(wgu.at[slot, :, pl.ds(wide, wide)], load_u.at[slot])

        @pl.when(jnp.logical_or(layer > 0, chunk > 0))
        def _():
            for copy in results(layer, chunk, part):
                copy.wait()

        def some(i, _):
            at = pl.ds(pl.multiple_of(part * half + i * step, step), step)
            out = pl.ds(pl.multiple_of(i * step, step), step)
            rows = a[at, :]
            both = jnp.dot(rows, wgu[slot], preferred_element_type=jnp.float32)
            gate, up = both[:, :wide], both[:, wide:]
            g_out[part, out, :] = gate
            u_out[part, out, :] = up
            on = (gate * jax.nn.sigmoid(gate) * up).astype(BF)
            hid[at, pl.ds(pl.multiple_of(chunk * wide, wide), wide)] = on
            t_out[part, :, out] = on.T
            return 0

        lax.fori_loop(0, half // step, some, 0)
        for copy in results(layer, chunk, part):
            copy.start()

    def down(layer, chunk):
        slot = chunk % 2
        arrived(wd.at[slot], load_d.at[slot])
        columns = pl.ds(pl.multiple_of(chunk * deep, deep), deep)

        def some(i, _):
            at = pl.ds(pl.multiple_of(i * step, step), step)
            y = jnp.dot(hid[at, :], wd[slot], preferred_element_type=jnp.float32).astype(BF)
            h[at, columns] = h[at, columns] + y
            return 0

        lax.fori_loop(0, tokens // step, some, 0)

    def states(layer):
        return (
            pltpu.make_async_copy(h, h_hbm.at[layer], io_sem.at[0]),
            pltpu.make_async_copy(a_t, at_hbm.at[layer], io_sem.at[1]),
        )

    def comm(t):
        for_unit(t, stage_one)
        for_unit(t - SECOND, stage_two)
        for_unit(t - THIRD, stage_three)
        for_unit(t - FOURTH, stage_four)
        for_unit(t - READY, ready)

    fetch = pltpu.make_async_copy(x_hbm, h, io_sem.at[0])
    fetch.start()
    fetch.wait()
    norm()
    for copy in states(0):
        copy.start()

    def tick(t, _):
        comm(t)
        u = t - READY - 1
        layer, r = u // per, u % per
        ok = jnp.logical_and(u >= 0, u < units)

        @pl.when(jnp.logical_and(ok, jnp.logical_and(r >= 1, r <= 2 * ups)))
        def _():
            gate_up(layer, (r - 1) // 2, (r - 1) % 2)

        @pl.when(jnp.logical_and(ok, jnp.logical_and(layer + 1 < layers, r >= 2 * ups)))
        def _():
            @pl.when(r == 2 * ups)
            def _():
                for copy in states(layer):
                    copy.wait()

            down(layer, r - 2 * ups)

            @pl.when(r == per - 1)
            def _():
                norm()
                for copy in states(layer + 1):
                    copy.start()

        return 0

    lax.fori_loop(0, units + READY + 1, tick, 0)
    for copy in (*results(layers - 1, ups - 1, 0), *results(layers - 1, ups - 1, 1), *states(layers - 1)):
        copy.wait()

    def finish(t, _):
        for_unit(t, all_sent)
        return 0

    lax.fori_loop(0, units, finish, 0)


def forward(x, w_gate, w_up, w_down, n):
    layers, _, ff = w_gate.shape
    tokens, d = x.shape
    wide, deep = WIDE, DEEP
    units = layers * (2 * (ff // wide) + d // deep)
    half = tokens // 2
    any_space = pl.BlockSpec(memory_space=pl.ANY)
    shape = jax.ShapeDtypeStruct
    out_shape = (
        shape((layers, tokens, ff), jnp.float32),
        shape((layers, tokens, ff), jnp.float32),
        shape((layers, ff, tokens), BF),
        shape((layers, d, tokens), BF),
        shape((layers, tokens, d), BF),
        shape((layers, d, ff), BF),
        shape((layers, d, ff), BF),
        shape((layers, ff, d), BF),
    )
    return pl.pallas_call(
        functools.partial(forward_kernel, n, wide, deep),
        out_shape=out_shape,
        in_specs=[any_space] * 4,
        out_specs=[any_space] * len(out_shape),
        scratch_shapes=[
            pltpu.VMEM((tokens, d), BF),
            pltpu.VMEM((tokens, d), BF),
            pltpu.VMEM((tokens, ff), BF),
            pltpu.VMEM((2, d, 2 * wide), BF),
            pltpu.VMEM((2, ff, deep), BF),
            pltpu.VMEM((2, half, wide), jnp.float32),
            pltpu.VMEM((2, half, wide), jnp.float32),
            pltpu.VMEM((2, wide, half), BF),
            pltpu.VMEM((d, tokens), BF),
            pltpu.SemaphoreType.DMA((units, 6)),
            pltpu.SemaphoreType.DMA((units,)),
            pltpu.SemaphoreType.DMA((units,)),
            pltpu.SemaphoreType.DMA((units,)),
            pltpu.SemaphoreType.DMA((2,)),
            pltpu.SemaphoreType.DMA((2,)),
            pltpu.SemaphoreType.DMA((2,)),
            pltpu.SemaphoreType.DMA((2, 3)),
            pltpu.SemaphoreType.DMA((2,)),
        ],
        compiler_params=pltpu.CompilerParams(collective_id=0, has_side_effects=True, vmem_limit_bytes=62 * 2**20),
        cost_estimate=pl.CostEstimate(flops=10 * tokens * d * ff, bytes_accessed=4 * layers * tokens * ff * 4, transcendentals=0),
    )(x, w_gate, w_up, w_down)


SUM_CHIP, SUM_NEAR, SUM_ALL = 1, 3, 5
HELD, FAR, NEAR = SUM_ALL + 1, SUM_NEAR - SUM_CHIP + 1, SUM_ALL - SUM_NEAR + 1


def backward_kernel(n, dy_hbm, h_hbm, at_hbm, ht_hbm, g_hbm, u_hbm, wg_hbm, wu_hbm, wd_hbm, gg_hbm, gu_hbm, gd_hbm, factor_out,
                    left, right, da, wd, wgu, gin, uin, hin, acc, sb, rb, sf, rh, sn, rn, so, sq, sqs,
                    left_sem, wd_sem, wgu_sem, gin_sem, hin_sem, out_sem, sb_sem, rb_sem, sf_sem, rh_sem, sn_sem, rn_sem,
                    free_b, free_h, free_n, sq_sem):
    layers, ff = g_hbm.shape[0], g_hbm.shape[2]
    tokens, d = dy_hbm.shape
    chips = n // 2
    part, wide = so.shape[1] // 2, so.shape[2]
    chunks, downs = ff // wide, ff // n // part
    splits = d // n // part
    per = downs + chunks * splits
    units = layers * per
    rep, me = lax.axis_index("rep"), lax.axis_index("dp")
    chip, core = me // 2, me % 2
    device = lambda c, k: (rep, (c % chips) * 2 + k)
    ahead, behind, beside = device(chip + 1, core), device(chip + chips - 1, core), device(chip, 1 - core)
    rows = 256

    barrier = pltpu.get_barrier_semaphore()

    def greet(i, _):
        pl.semaphore_signal(barrier, inc=1, device_id=(rep, (me + i) % n), device_id_type=MESH)
        return 0

    lax.fori_loop(1, n, greet, 0)
    pl.semaphore_wait(barrier, n - 1)

    def arrived(ref, sem):
        pltpu.make_async_copy(ref, ref, sem).wait()

    def send(src, dst, send_sem, recv_sem, to):
        pltpu.make_async_remote_copy(src_ref=src, dst_ref=dst, send_sem=send_sem, recv_sem=recv_sem, device_id=to, device_id_type=MESH).start()

    def signal(sem, to):
        pl.semaphore_signal(sem, inc=1, device_id=to, device_id_type=MESH)

    def place(u):
        return layers - 1 - u // per, u % per

    def load_left(src, layer, block, start, slot):
        for e in range(2):
            for q in range(chips):
                j = ((chip + q) % chips) * 2 + (core if e == 0 else 1 - core)
                at = pl.ds(pl.multiple_of(j * block + start, 16), part)
                pltpu.make_async_copy(src.at[layer, at, :], left.at[slot, pl.ds((e * chips + q) * part, part), :], left_sem.at[slot]).start()

    def left_ready(slot):
        arrived(left.at[slot], left_sem.at[slot])

    def chunk_columns(chunk):
        return pl.ds(pl.multiple_of(chunk * wide, wide), wide)

    def load_wd(layer, chunk):
        return pltpu.make_async_copy(wd_hbm.at[layer, chunk_columns(chunk), :], wd, wd_sem)

    def load_wgu(layer, chunk):
        return (
            pltpu.make_async_copy(wg_hbm.at[layer, :, chunk_columns(chunk)], wgu.at[:, pl.ds(0, wide)], wgu_sem.at[0]),
            pltpu.make_async_copy(wu_hbm.at[layer, :, chunk_columns(chunk)], wgu.at[:, pl.ds(wide, wide)], wgu_sem.at[1]),
        )

    def load_gate_up(layer, chunk, i):
        at = pl.ds(pl.multiple_of(i * rows, rows), rows)
        slot = i % 2
        return (
            pltpu.make_async_copy(g_hbm.at[layer, at, chunk_columns(chunk)], gin.at[slot], gin_sem.at[slot, 0]),
            pltpu.make_async_copy(u_hbm.at[layer, at, chunk_columns(chunk)], uin.at[slot], gin_sem.at[slot, 1]),
        )

    def load_h(layer, i):
        return pltpu.make_async_copy(h_hbm.at[layer, pl.ds(pl.multiple_of(i * rows, rows), rows), :], hin.at[i % 2], hin_sem.at[i % 2])

    def by_hidden(layer, chunk):
        load_wd(layer, chunk).wait()

        def some(i, _):
            at = pl.ds(pl.multiple_of(i * rows, rows), rows)
            slot = i % 2
            for copy in load_gate_up(layer, chunk, i):
                copy.wait()
            by = dot(right[0, at, :], wd[...], ((1,), (1,))).astype(BF).astype(jnp.float32)
            gate, up = gin[slot], uin[slot]
            on = jax.nn.sigmoid(gate)
            right[1, at, pl.ds(0, wide)] = (by * up * (on + gate * on * (1.0 - on))).astype(BF)
            right[1, at, pl.ds(wide, wide)] = (by * (gate * on)).astype(BF)

            @pl.when(i + 2 < tokens // rows)
            def _():
                for copy in load_gate_up(layer, chunk, i + 2):
                    copy.start()

            return 0

        lax.fori_loop(0, tokens // rows, some, 0)

    def by_normed(chunk):
        def some(i, _):
            at = pl.ds(pl.multiple_of(i * rows, rows), rows)
            by = dot(right[1, at, :], wgu[...], ((1,), (1,)))
            da[at, :] = jnp.where(chunk == 0, 0.0, da[at, :]) + by
            return 0

        lax.fori_loop(0, tokens // rows, some, 0)

    def by_states(layer):
        def some(i, _):
            at = pl.ds(pl.multiple_of(i * rows, rows), rows)
            load_h(layer, i).wait()
            w = hin[i % 2].astype(jnp.float32)
            by = da[at, :].astype(BF).astype(jnp.float32)
            scale = lax.rsqrt(jnp.mean(w * w, -1, keepdims=True) + 1e-6)
            back = by * scale - w * (scale * scale * scale * jnp.mean(by * w, -1, keepdims=True))
            right[0, at, :] = right[0, at, :] + back.astype(BF)

            @pl.when(i + 2 < tokens // rows)
            def _():
                load_h(layer, i + 2).start()

            return 0

        lax.fori_loop(0, tokens // rows, some, 0)

    def products(u, lefts, rights):
        two, held = u % 2, u % HELD

        @pl.when(u >= 2)
        def _():
            arrived(sb.at[two], sb_sem.at[two])

        def some(i, _):
            e = 1 - i
            lhs = left[lefts, pl.ds(pl.multiple_of(e * chips * part, 16), chips * part), :]
            by = dot(lhs, right[rights], ((1,), (0,)))
            for side in range(2):
                for q in range(chips):
                    block = by[q * part : (q + 1) * part, side * wide : (side + 1) * wide]

                    @pl.when(e == 1)
                    def _():
                        sb[two, q, side * part : (side + 1) * part, :] = block.astype(BF)

                    @pl.when(e == 0)
                    def _():
                        acc[held, q, side * part : (side + 1) * part, :] = block

            @pl.when(e == 1)
            def _():
                @pl.when(u >= 2)
                def _():
                    pl.semaphore_wait(free_b, 1)

                send(sb.at[two], rb.at[two], sb_sem.at[two], rb_sem.at[two], beside)

            return 0

        lax.fori_loop(0, 2, some, 0)

    first, second = pl.ds(0, part), pl.ds(part, part)

    def sum_chip(u):
        two, held, far = u % 2, u % HELD, u % FAR
        arrived(rb.at[two], rb_sem.at[two])

        @pl.when(u >= FAR)
        def _():
            arrived(sf.at[far, first], sf_sem.at[far, 0])
            arrived(sf.at[far, second], sf_sem.at[far, 1])

        sf[far] = (acc[held, 2] + rb[two, 2].astype(jnp.float32)).astype(BF)

        @pl.when(u >= FAR)
        def _():
            pl.semaphore_wait(free_h.at[0], 1)
            pl.semaphore_wait(free_h.at[1], 1)

        send(sf.at[far, first], rh.at[far, first], sf_sem.at[far, 0], rh_sem.at[far, 0], ahead)
        send(sf.at[far, second], rh.at[far, second], sf_sem.at[far, 1], rh_sem.at[far, 1], behind)
        for q in (1, 3, 0):
            acc[held, q] = acc[held, q] + rb[two, q].astype(jnp.float32)

        @pl.when(u < units - 2)
        def _():
            signal(free_b, beside)

    def sum_near(u):
        held, far, near = u % HELD, u % FAR, u % NEAR
        arrived(rh.at[far, first], rh_sem.at[far, 0])
        arrived(rh.at[far, second], rh_sem.at[far, 1])

        @pl.when(u >= NEAR)
        def _():
            arrived(sn.at[near, 0], sn_sem.at[near, 0])
            arrived(sn.at[near, 1], sn_sem.at[near, 1])

        sn[near, 0, first, :] = (acc[held, 1, first, :] + rh[far, first, :].astype(jnp.float32)).astype(BF)
        sn[near, 0, second, :] = acc[held, 1, second, :].astype(BF)
        sn[near, 1, first, :] = acc[held, 3, first, :].astype(BF)
        sn[near, 1, second, :] = (acc[held, 3, second, :] + rh[far, second, :].astype(jnp.float32)).astype(BF)

        @pl.when(u < units - FAR)
        def _():
            signal(free_h.at[0], behind)
            signal(free_h.at[1], ahead)

        @pl.when(u >= NEAR)
        def _():
            pl.semaphore_wait(free_n.at[0], 1)
            pl.semaphore_wait(free_n.at[1], 1)

        send(sn.at[near, 0], rn.at[near, 0], sn_sem.at[near, 0], rn_sem.at[near, 0], ahead)
        send(sn.at[near, 1], rn.at[near, 1], sn_sem.at[near, 1], rn_sem.at[near, 1], behind)

    def for_results(u, do):
        layer, r = place(u)
        two = u % 2

        @pl.when(r < downs)
        def _():
            at = pl.ds(pl.multiple_of(r * part, 16), part)
            do(pltpu.make_async_copy(so.at[two, first], gd_hbm.at[layer, at, pl.ds(0, wide)], out_sem.at[two, 0]))
            do(pltpu.make_async_copy(so.at[two, second], gd_hbm.at[layer, at, pl.ds(wide, wide)], out_sem.at[two, 1]))

        @pl.when(r >= downs)
        def _():
            chunk, z = (r - downs) // splits, (r - downs) % splits
            at = pl.ds(pl.multiple_of(z * part, 16), part)
            do(pltpu.make_async_copy(so.at[two, first], gg_hbm.at[layer, at, chunk_columns(chunk)], out_sem.at[two, 0]))
            do(pltpu.make_async_copy(so.at[two, second], gu_hbm.at[layer, at, chunk_columns(chunk)], out_sem.at[two, 1]))

    def sum_all(u):
        held, near, two = u % HELD, u % NEAR, u % 2
        arrived(rn.at[near, 0], rn_sem.at[near, 0])
        arrived(rn.at[near, 1], rn_sem.at[near, 1])

        @pl.when(u >= 2)
        def _():
            arrived(so.at[two, first], out_sem.at[two, 0])
            arrived(so.at[two, second], out_sem.at[two, 1])

        g = (acc[held, 0] + rn[near, 0].astype(jnp.float32) + rn[near, 1].astype(jnp.float32)).astype(BF)
        so[two] = g
        wide_g = g.astype(jnp.float32)
        sq[...] += jnp.sum((wide_g * wide_g).reshape(2 * part // 8, 8, wide), axis=0)

        @pl.when(u < units - NEAR)
        def _():
            signal(free_n.at[0], behind)
            signal(free_n.at[1], ahead)

        for_results(u, lambda copy: copy.start())

    def when_unit(u, body):
        @pl.when(jnp.logical_and(u >= 0, u < units))
        def _():
            body(u)

    def compute(u):
        layer, r = place(u)

        @pl.when(r == 0)
        def _():
            for z in range(splits):
                load_left(at_hbm, layer, d // n, z * part, 2 + z)
            load_wd(layer, 0).start()

        @pl.when(r + 1 < downs)
        def _():
            load_left(ht_hbm, layer, ff // n, (r + 1) * part, (r + 1) % 2)

        @pl.when(jnp.logical_and(u + 1 < units, r == per - 1))
        def _():
            load_left(ht_hbm, layer - 1, ff // n, 0, 0)

        after_down = r - downs
        chunk, z = after_down // splits, after_down % splits

        @pl.when(jnp.logical_and(after_down + 1 >= 0, jnp.logical_and((after_down + 1) % splits == 0, r + 1 < per)))
        def _():
            for i in range(2):
                for copy in load_gate_up(layer, (after_down + 1) // splits, i):
                    copy.start()

        @pl.when(r < downs)
        def _():
            left_ready(r % 2)

        @pl.when(jnp.logical_and(after_down >= 0, z == 0))
        def _():
            @pl.when(layer > 0)
            def _():
                for copy in load_wgu(layer, chunk):
                    copy.start()

            by_hidden(layer, chunk)

            @pl.when(chunk + 1 < chunks)
            def _():
                load_wd(layer, chunk + 1).start()

        for first_z in range(splits):

            @pl.when(after_down == first_z)
            def _():
                left_ready(2 + first_z)

        products(u, jnp.where(r < downs, r % 2, 2 + z), jnp.where(r < downs, 0, 1))

        @pl.when(jnp.logical_and(layer > 0, jnp.logical_and(after_down >= 0, z == splits - 1)))
        def _():
            @pl.when(r == per - 1)
            def _():
                load_h(layer, 0).start()
                load_h(layer, 1).start()

            for copy in load_wgu(layer, chunk):
                copy.wait()
            by_normed(chunk)

            @pl.when(r == per - 1)
            def _():
                by_states(layer)

    sq[...] = jnp.zeros_like(sq)
    fetch = pltpu.make_async_copy(dy_hbm, right.at[0], wd_sem)
    fetch.start()
    load_left(ht_hbm, layers - 1, ff // n, 0, 0)
    fetch.wait()

    def tick(t, _):
        when_unit(t - SUM_ALL, sum_all)
        when_unit(t - SUM_NEAR, sum_near)
        when_unit(t - SUM_CHIP, sum_chip)
        when_unit(t, compute)
        return 0

    lax.fori_loop(0, units + SUM_ALL, tick, 0)

    for two in range(2):
        arrived(so.at[two, first], out_sem.at[two, 0])
        arrived(so.at[two, second], out_sem.at[two, 1])
        arrived(sb.at[two], sb_sem.at[two])
    for far in range(FAR):
        arrived(sf.at[far, first], sf_sem.at[far, 0])
        arrived(sf.at[far, second], sf_sem.at[far, 1])
    for near in range(NEAR):
        arrived(sn.at[near, 0], sn_sem.at[near, 0])
        arrived(sn.at[near, 1], sn_sem.at[near, 1])

    some = sq[:, 0:128]
    for i in range(1, wide // 128):
        some = some + sq[:, i * 128 : (i + 1) * 128]
    sqs[me] = some

    def tell(i, _):
        send(sqs.at[me], sqs.at[me], sq_sem.at[0], sq_sem.at[1], (rep, (me + i) % n))
        return 0

    lax.fori_loop(1, n, tell, 0)
    others = sqs.at[pl.ds(0, n - 1)]
    arrived(others, sq_sem.at[1])
    arrived(others, sq_sem.at[0])
    total = sqs[0]
    for i in range(1, n):
        total = total + sqs[i]
    mean = jnp.sum(total, keepdims=True) / (3 * layers * d * ff)
    factor_out[...] = jnp.broadcast_to(jnp.minimum(1.0, 0.5 * lax.rsqrt(mean + 1e-30)), factor_out.shape)


def backward(dy, h, a_t, hid_t, gate, up, whole, n):
    layers, tokens, ff = gate.shape
    d = dy.shape[1]
    wide, part = WIDE, d // n // 2
    any_space = pl.BlockSpec(memory_space=pl.ANY)
    shape, vmem, dma = jax.ShapeDtypeStruct, pltpu.VMEM, pltpu.SemaphoreType.DMA
    block = (2 * part, wide)
    return pl.pallas_call(
        functools.partial(backward_kernel, n),
        out_shape=(
            shape((layers, d // n, ff), BF),
            shape((layers, d // n, ff), BF),
            shape((layers, ff // n, d), BF),
            shape((8, 128), jnp.float32),
        ),
        in_specs=[any_space] * 9,
        out_specs=[any_space] * 3 + [pl.BlockSpec(memory_space=pltpu.VMEM)],
        scratch_shapes=[
            vmem((4, n * part, tokens), BF),
            vmem((2, tokens, d), BF),
            vmem((tokens, d), jnp.float32),
            vmem((wide, d), BF),
            vmem((d, 2 * wide), BF),
            vmem((2, 256, wide), jnp.float32),
            vmem((2, 256, wide), jnp.float32),
            vmem((2, 256, d), BF),
            vmem((HELD, n // 2, *block), jnp.float32),
            vmem((2, n // 2, *block), BF),
            vmem((2, n // 2, *block), BF),
            vmem((FAR, *block), BF),
            vmem((FAR, *block), BF),
            vmem((NEAR, 2, *block), BF),
            vmem((NEAR, 2, *block), BF),
            vmem((2, *block), BF),
            vmem((8, wide), jnp.float32),
            vmem((n, 8, 128), jnp.float32),
            dma((4,)),
            dma(()),
            dma((2,)),
            dma((2, 2)),
            dma((2,)),
            dma((2, 2)),
            dma((2,)),
            dma((2,)),
            dma((FAR, 2)),
            dma((FAR, 2)),
            dma((NEAR, 2)),
            dma((NEAR, 2)),
            pltpu.SemaphoreType.REGULAR,
            pltpu.SemaphoreType.REGULAR((2,)),
            pltpu.SemaphoreType.REGULAR((2,)),
            dma((2,)),
        ],
        compiler_params=pltpu.CompilerParams(collective_id=1, has_side_effects=True, vmem_limit_bytes=63 * 2**20),
        cost_estimate=pl.CostEstimate(flops=20 * tokens * d * ff, bytes_accessed=4 * layers * tokens * ff * 4, transcendentals=0),
    )(dy, h, a_t, hid_t, gate, up, *whole)


def solution(mesh):
    n = mesh.shape["dp"]

    def step(x, dy, *arrays):
        weights, m, v = (arrays[i : i + 3] for i in (0, 3, 6))
        gate, up, hid_t, a_t, h, *whole = forward(x[0], *weights, n)
        *gradients, factor = backward(dy[0], h, a_t, hid_t, gate, up, whole, n)
        factor = factor[0, 0]
        new = [adamw(w.astype(jnp.float32), m, v, g.astype(jnp.float32) * factor) for w, m, v, g in zip(weights, m, v, gradients, strict=True)]
        return tuple(one[which] for which in range(3) for one in new)

    states, cut = P(("rep", "dp"), None, None), P(None, "dp", None)
    return jax.shard_map(
        step,
        mesh=mesh,
        in_specs=(states, states) + (cut,) * 9,
        out_specs=(P("rep", "dp", None),) * 9,
        check_vma=False,
    )
```

time: 997 us -> 729 us (0.73)
  Pallas kernels: 0 us -> 693 us
  matrix products: 550 us -> 0 us
  waiting for transfers between devices: 325 us -> 0 us
  other arithmetic: 57.8 us -> 27.9 us
  local copies, waits for them, and re-layouts: 26.8 us -> 5.55 us
  between operations: 17.6 us -> 0.67 us
  blocking collectives: 13.8 us -> 0 us
    pallas_call x0 -> x2, Pallas kernels: none -> 693 us  [the longest x1 418 us: backward(): pl.pallas_call(functools.partial(backward_kernel, n), out_shape=(shape((l...]
    dot_general x15 -> x0, matrix products: 550 us -> none  [the longest x5 197 us: layer(): gate = jnp.dot(a, w['w_gate'], preferred_element_type=jnp.float32)]
    all_gather x6 -> x0, waiting for transfers between devices: 166 us -> none  [fetched(): lax.all_gather(w[number], 'dp', axis=0, tiled=True)]
    reduce_scatter x6 -> x0, waiting for transfers between devices: 157 us -> none  [step(): lax.psum_scatter(by_w[name], 'dp', scatter_dimension=0, tiled=True)]
    reduce_sum x4 -> x0, other arithmetic: 15.3 us -> none  [the longest x3 11.8 us: step(): squares = lax.psum(sum((jnp.sum(g * g) for g in gradients)), 'dp')]
    psum x1 -> x0, blocking collectives: 13.8 us -> none  [step(): squares = lax.psum(sum((jnp.sum(g * g) for g in gradients)), 'dp')]
    unnamed x30 -> x8, local copies, waits for them, and re-layouts: 17.7 us -> 4.37 us
    add_any x1 -> x0, other arithmetic: 12.4 us -> none  [normed(): wide = h.astype(jnp.float32)]
  transfers between devices with their start and end apart: 12 -> 0, of which waited for: 9 -> 0; matrix products, arithmetic and copies ran while one was open for 43% -> 0% of each run, Pallas kernels for 0% -> 0%
where the time goes in v1:
time: 729 us; the launch traced here: 727 us
  Pallas kernels  693 us (95%)
  other arithmetic  27.9 us (4%)
    pallas_call x1, Pallas kernels, backward(): pl.pallas_call(functools.partial(backward_kernel, n), out_shape=(shape((l...  418 us
    pallas_call x1, Pallas kernels, forward(): pl.pallas_call(functools.partial(forward_kernel, n, wide, deep), out_shap...  275 us
    convert_element_type x2, other arithmetic, adamw(): return ((w - 0.02 * step).astype(BF), m, v)  27.9 us

profile of v1, /device:TPU:113, one launch (start us, length us, event | category | flops | bytes accessed | tf_op | source)
XLA Modules:
  0.0 727.4 jit_solution(12671603113134360672)
XLA Ops:
  0.6 275.5 %shard_map.178 = (f32[2,2048,4480]{2,1,0:T(8,128)}, f32[2,2048,4480]{2,1,0:T(8,128)}, bf16[2,4480,2048]{2,1,0:T(8,128)(2,1)}, bf16[2,1280,2048]{2,1,0:T(8,128)(2...) custom-call(bf16[2048,1280]{1,0:T(8,128)(2,1)} %bitcast.3, ...), custom_call_target="tpu_custom_call" | custom-call | flops 117440512000 | bytes 293601280 | tf_op jit(solution)/shard_map/pallas_call | solution.py:283
  276.1 417.8 %shard_map.179 = (bf16[2,160,4480]{2,1,0:T(8,128)(2,1)}, bf16[2,160,4480]{2,1,0:T(8,128)(2,1)}, bf16[2,560,1280]{2,1,0:T(8,128)(2,1)}, f32[8,128]{1,0:T(8,128)}) custom-call(bf16[2048,1280]{1,0:T(8,128)(2,1)} %bitcast.4, bf16[2,2048,1280]{2,1,0:T(8,128)(2,1)} %get-tuple-element.21.h_hbm, bf16[2,1280,2048]{2,1,0:T(8,128)(2,1)} %get-tuple-element.22.at_hbm, ...), custom_call_target="tpu_custom_call" | custom-call | flops 234881024000 | bytes 293601280 | tf_op jit(solution)/shard_map/pallas_call | solution.py:692
  693.9 1.2 slice.3
  695.1 0.0 copy-start
  695.1 0.0 copy-start.1
  695.1 0.0 copy-start.2
  695.1 0.0 copy-start.3
  695.1 13.3 %fusion.8 = (bf16[2,560,1280]{2,1,0:T(8,128)(2,1)}, f32[2,560,1280]{2,1,0:T(8,128)}, f32[2,560,1280]{2,1,0:T(8,128)}) fusion(bf16[2,560,1280]{2,1,0:T(8,128)(2,1)} %wd_hbm.1, f32[]{:T(128)} %bitcast.2, bf16[2,560,1280]{2,1,0:T(8,128)(2,1)} %get-tuple-element.32, f32[2,560,1280]{2,1,0:T(8,128)} %param.21, f32[2,560,1280]{2,1,0:T(8,128)} %param.18), kind=kLoop, calls=%fused_computation.17 | loop fusion | flops 24371200 | bytes 31539204 | tf_op jit(solution)/shard_map/convert_element_type | solution.py:22
  708.4 0.0 copy-done
  708.4 1.1 copy-done.1
  709.5 1.6 copy-done.2
  711.1 1.6 copy-done.3
  712.8 14.6 %fusion.2 = (bf16[2,160,4480]{2,1,0:T(8,128)(2,1)}, f32[2,160,4480]{2,1,0:T(8,128)}, f32[2,160,4480]{2,1,0:T(8,128)}, bf16[2,160,4480]{2,1,0:T(8,128)(2,1)}, f32...) fusion(bf16[2,160,4480]{2,1,0:T(8,128)(2,1)} %wg_hbm.1, f32[]{:T(128)} %bitcast.2, ...), kind=kLoop, calls=%fused_computation.11 | loop fusion | flops 48742400 | bytes 63078404 | tf_op jit(solution)/shard_map/convert_element_type | solution.py:22
Async XLA Ops:
  695.1 13.3 %copy-start = (f32[2,160,4480]{2,1,0:T(8,128)S(1)}, f32[2,160,4480]{2,1,0:T(8,128)}, u32[]{:S(2)}) copy-start(f32[2,160,4480]{2,1,0:T(8,128)} %param.19) | copy-start | bytes 17203204
  695.1 14.4 %copy-start.1 = (f32[2,160,4480]{2,1,0:T(8,128)S(1)}, f32[2,160,4480]{2,1,0:T(8,128)}, u32[]{:S(2)}) copy-start(f32[2,160,4480]{2,1,0:T(8,128)} %param.16) | copy-start | bytes 17203204
  695.1 16.0 %copy-start.2 = (f32[2,160,4480]{2,1,0:T(8,128)S(1)}, f32[2,160,4480]{2,1,0:T(8,128)}, u32[]{:S(2)}) copy-start(f32[2,160,4480]{2,1,0:T(8,128)} %param.20) | copy-start | bytes 17203204
  695.1 17.6 %copy-start.3 = (f32[2,160,4480]{2,1,0:T(8,128)S(1)}, f32[2,160,4480]{2,1,0:T(8,128)}, u32[]{:S(2)}) copy-start(f32[2,160,4480]{2,1,0:T(8,128)} %param.17) | copy-start | bytes 17203204

commit v2 on v1

--- a/solution.py
+++ b/solution.py
@@ -23,20 +23,22 @@
 
 
 MESH = pl.DeviceIdType.MESH
-SECOND, THIRD, FOURTH, READY = 1, 2, 3, 4
+SECOND, THIRD, FOURTH, READY = 2, 4, 6, 7
+
+PASSING = THIRD + 1
 
 
 def pieces(rows):
-    theirs = rows * 3 // 10 // 16 * 16
+    theirs = rows // 3 // 16 * 16
     return rows - theirs, theirs
 
 
 def forward_kernel(n, wide, deep, x_hbm, wg_hbm, wu_hbm, wd_hbm, g_hbm, u_hbm, ht_hbm, at_hbm, h_hbm, fg_hbm, fu_hbm, fd_hbm,
-                   h, a, hid, wgu, wd, g_out, u_out, t_out, a_t, recv, whole, local, sent, load_g, load_u, load_d, out_sem, io_sem):
+                   h, a, hid, wgu, wd, g_out, u_out, t_out, a_t, pass_wide, pass_deep, recv, whole, local, sent, load_g, load_u, load_d, out_sem, io_sem, pass_sem):
     layers, ff = wg_hbm.shape[0], wg_hbm.shape[2]
     tokens, d = x_hbm.shape
     chips, half = n // 2, tokens // 2
-    step = half // 4
+    step = half // 2
     ups, downs = ff // wide, d // deep
     per = 2 * ups + downs
     units = layers * per
@@ -86,7 +88,8 @@
         send(unit, own(start, mine), full(me * rows + start, mine), to_ahead, recv.at[unit, 0])
         send(unit, own(start, mine), full(me * rows + start, mine), to_behind, recv.at[unit, 1])
         send(unit, own(0, rows), full(me * rows, rows), to_beside, whole.at[unit])
-        pltpu.make_async_copy(own(0, rows), full(me * rows, rows), local.at[unit]).start()
+        bounce = (pass_deep if kind == 2 else pass_wide).at[unit % PASSING]
+        pltpu.make_async_copy(own(0, rows), bounce, pass_sem.at[unit % PASSING]).start()
 
     def onward(unit, rows, full, block, pair_sem):
         mine, theirs = pieces(rows)
@@ -102,6 +105,9 @@
 
     def stage_two(kind, unit, layer, chunk):
         rows, _, full = unit_views(kind, layer, chunk)
+        bounce = (pass_deep if kind == 2 else pass_wide).at[unit % PASSING]
+        arrived(bounce, pass_sem.at[unit % PASSING])
+        pltpu.make_async_copy(bounce, full(me * rows, rows), local.at[unit]).start()
         mine, theirs = pieces(rows)
         first = full(behind * rows + parity * theirs, mine)
         arrived(first, recv.at[unit, 0])
@@ -111,8 +117,9 @@
         onward(unit, rows, full, ahead, recv.at[unit, 4])
 
     def stage_three(kind, unit, layer, chunk):
-        rows, _, full = unit_views(kind, layer, chunk)
+        rows, own, full = unit_views(kind, layer, chunk)
         mine, theirs = pieces(rows)
+        arrived(own(0, rows), local.at[unit])
         arrived(full(across * rows + parity * theirs, mine), recv.at[unit, 2])
         onward(unit, rows, full, across, recv.at[unit, 5])
         from_pair(unit, rows, full, behind, recv.at[unit, 3])
@@ -123,9 +130,8 @@
         from_pair(unit, rows, full, across, recv.at[unit, 5])
 
     def ready(kind, unit, layer, chunk):
-        rows, own, full = unit_views(kind, layer, chunk)
+        rows, _, full = unit_views(kind, layer, chunk)
         arrived(full(0, chips * rows), whole.at[unit])
-        arrived(own(0, rows), local.at[unit])
         slot = chunk % 2
         if kind == 0:
             pltpu.make_async_copy(full(0, d), wgu.at[slot, :, pl.ds(0, wide)], load_g.at[slot]).start()
@@ -219,13 +225,17 @@
 
     fetch = pltpu.make_async_copy(x_hbm, h, io_sem.at[0])
     fetch.start()
-    fetch.wait()
-    norm()
-    for copy in states(0):
-        copy.start()
 
     def tick(t, _):
         comm(t)
+
+        @pl.when(t == SECOND)
+        def _():
+            fetch.wait()
+            norm()
+            for copy in states(0):
+                copy.start()
+
         u = t - READY - 1
         layer, r = u // per, u % per
         ok = jnp.logical_and(u >= 0, u < units)
@@ -295,6 +305,8 @@
             pltpu.VMEM((2, half, wide), jnp.float32),
             pltpu.VMEM((2, wide, half), BF),
             pltpu.VMEM((d, tokens), BF),
+            pltpu.VMEM((PASSING, d // n, wide), BF),
+            pltpu.VMEM((PASSING, ff // n, deep), BF),
             pltpu.SemaphoreType.DMA((units, 6)),
             pltpu.SemaphoreType.DMA((units,)),
             pltpu.SemaphoreType.DMA((units,)),
@@ -304,18 +316,19 @@
             pltpu.SemaphoreType.DMA((2,)),
             pltpu.SemaphoreType.DMA((2, 3)),
             pltpu.SemaphoreType.DMA((2,)),
+            pltpu.SemaphoreType.DMA((PASSING,)),
         ],
         compiler_params=pltpu.CompilerParams(collective_id=0, has_side_effects=True, vmem_limit_bytes=62 * 2**20),
         cost_estimate=pl.CostEstimate(flops=10 * tokens * d * ff, bytes_accessed=4 * layers * tokens * ff * 4, transcendentals=0),
     )(x, w_gate, w_up, w_down)
 
 
-SUM_CHIP, SUM_NEAR, SUM_ALL = 1, 3, 5
-HELD, FAR, NEAR = SUM_ALL + 1, SUM_NEAR - SUM_CHIP + 1, SUM_ALL - SUM_NEAR + 1
+SUM_CHIP, SUM_NEAR, SUM_ALL = 1, 4, 7
+FAR, NEAR = SUM_NEAR - SUM_CHIP + 1, SUM_ALL - SUM_NEAR + 1
 
 
 def backward_kernel(n, dy_hbm, h_hbm, at_hbm, ht_hbm, g_hbm, u_hbm, wg_hbm, wu_hbm, wd_hbm, gg_hbm, gu_hbm, gd_hbm, factor_out,
-                    left, right, da, wd, wgu, gin, uin, hin, acc, sb, rb, sf, rh, sn, rn, so, sq, sqs,
+                    left, right, da, wd, wgu, gin, uin, hin, acc_far, acc_near, acc_own, sb, rb, sf, rh, sn, rn, so, sq, sqs,
                     left_sem, wd_sem, wgu_sem, gin_sem, hin_sem, out_sem, sb_sem, rb_sem, sf_sem, rh_sem, sn_sem, rn_sem,
                     free_b, free_h, free_n, sq_sem):
     layers, ff = g_hbm.shape[0], g_hbm.shape[2]
@@ -330,7 +343,7 @@
     chip, core = me // 2, me % 2
     device = lambda c, k: (rep, (c % chips) * 2 + k)
     ahead, behind, beside = device(chip + 1, core), device(chip + chips - 1, core), device(chip, 1 - core)
-    rows = 256
+    rows, few = 512, 256
 
     barrier = pltpu.get_barrier_semaphore()
 
@@ -384,7 +397,7 @@
         )
 
     def load_h(layer, i):
-        return pltpu.make_async_copy(h_hbm.at[layer, pl.ds(pl.multiple_of(i * rows, rows), rows), :], hin.at[i % 2], hin_sem.at[i % 2])
+        return pltpu.make_async_copy(h_hbm.at[layer, pl.ds(pl.multiple_of(i * few, few), few), :], hin.at[i % 2], hin_sem.at[i % 2])
 
     def by_hidden(layer, chunk):
         load_wd(layer, chunk).wait()
@@ -420,7 +433,7 @@
 
     def by_states(layer):
         def some(i, _):
-            at = pl.ds(pl.multiple_of(i * rows, rows), rows)
+            at = pl.ds(pl.multiple_of(i * few, few), few)
             load_h(layer, i).wait()
             w = hin[i % 2].astype(jnp.float32)
             by = da[at, :].astype(BF).astype(jnp.float32)
@@ -428,53 +441,42 @@
             back = by * scale - w * (scale * scale * scale * jnp.mean(by * w, -1, keepdims=True))
             right[0, at, :] = right[0, at, :] + back.astype(BF)
 
-            @pl.when(i + 2 < tokens // rows)
+            @pl.when(i + 2 < tokens // few)
             def _():
                 load_h(layer, i + 2).start()
 
             return 0
 
-        lax.fori_loop(0, tokens // rows, some, 0)
+        lax.fori_loop(0, tokens // few, some, 0)
 
     def products(u, lefts, rights):
-        two, held = u % 2, u % HELD
+        two = u % 2
 
         @pl.when(u >= 2)
         def _():
             arrived(sb.at[two], sb_sem.at[two])
 
-        def some(i, _):
-            e = 1 - i
-            lhs = left[lefts, pl.ds(pl.multiple_of(e * chips * part, 16), chips * part), :]
-            by = dot(lhs, right[rights], ((1,), (0,)))
-            for side in range(2):
-                for q in range(chips):
-                    block = by[q * part : (q + 1) * part, side * wide : (side + 1) * wide]
-
-                    @pl.when(e == 1)
-                    def _():
-                        sb[two, q, side * part : (side + 1) * part, :] = block.astype(BF)
-
-                    @pl.when(e == 0)
-                    def _():
-                        acc[held, q, side * part : (side + 1) * part, :] = block
-
-            @pl.when(e == 1)
-            def _():
-                @pl.when(u >= 2)
-                def _():
-                    pl.semaphore_wait(free_b, 1)
-
-                send(sb.at[two], rb.at[two], sb_sem.at[two], rb_sem.at[two], beside)
-
-            return 0
-
-        lax.fori_loop(0, 2, some, 0)
+        by = dot(left[lefts], right[rights], ((1,), (0,)))
+        for side in range(2):
+            at, columns = pl.ds(side * part, part), slice(side * wide, (side + 1) * wide)
+            block = lambda k: by[k * part : (k + 1) * part, columns]
+            for q in range(chips):
+                sb[two, q, at, :] = block(chips + q).astype(BF)
+            acc_own[u % (SUM_ALL + 1), at, :] = block(0)
+            acc_near[u % (SUM_NEAR + 1), 0, at, :] = block(1)
+            acc_far[u % (SUM_CHIP + 1), at, :] = block(2)
+            acc_near[u % (SUM_NEAR + 1), 1, at, :] = block(3)
+
+        @pl.when(u >= 2)
+        def _():
+            pl.semaphore_wait(free_b, 1)
+
+        send(sb.at[two], rb.at[two], sb_sem.at[two], rb_sem.at[two], beside)
 
     first, second = pl.ds(0, part), pl.ds(part, part)
 
     def sum_chip(u):
-        two, held, far = u % 2, u % HELD, u % FAR
+        two, far, nearby, own = u % 2, u % FAR, u % (SUM_NEAR + 1), u % (SUM_ALL + 1)
         arrived(rb.at[two], rb_sem.at[two])
 
         @pl.when(u >= FAR)
@@ -482,7 +484,7 @@
             arrived(sf.at[far, first], sf_sem.at[far, 0])
             arrived(sf.at[far, second], sf_sem.at[far, 1])
 
-        sf[far] = (acc[held, 2] + rb[two, 2].astype(jnp.float32)).astype(BF)
+        sf[far] = (acc_far[u % (SUM_CHIP + 1)] + rb[two, 2].astype(jnp.float32)).astype(BF)
 
         @pl.when(u >= FAR)
         def _():
@@ -491,15 +493,16 @@
 
         send(sf.at[far, first], rh.at[far, first], sf_sem.at[far, 0], rh_sem.at[far, 0], ahead)
         send(sf.at[far, second], rh.at[far, second], sf_sem.at[far, 1], rh_sem.at[far, 1], behind)
-        for q in (1, 3, 0):
-            acc[held, q] = acc[held, q] + rb[two, q].astype(jnp.float32)
+        for i in range(2):
+            acc_near[nearby, i] = acc_near[nearby, i] + rb[two, 1 + 2 * i].astype(jnp.float32)
+        acc_own[own] = acc_own[own] + rb[two, 0].astype(jnp.float32)
 
         @pl.when(u < units - 2)
         def _():
             signal(free_b, beside)
 
     def sum_near(u):
-        held, far, near = u % HELD, u % FAR, u % NEAR
+        held, far, near = u % (SUM_NEAR + 1), u % FAR, u % NEAR
         arrived(rh.at[far, first], rh_sem.at[far, 0])
         arrived(rh.at[far, second], rh_sem.at[far, 1])
 
@@ -508,10 +511,10 @@
             arrived(sn.at[near, 0], sn_sem.at[near, 0])
             arrived(sn.at[near, 1], sn_sem.at[near, 1])
 
-        sn[near, 0, first, :] = (acc[held, 1, first, :] + rh[far, first, :].astype(jnp.float32)).astype(BF)
-        sn[near, 0, second, :] = acc[held, 1, second, :].astype(BF)
-        sn[near, 1, first, :] = acc[held, 3, first, :].astype(BF)
-        sn[near, 1, second, :] = (acc[held, 3, second, :] + rh[far, second, :].astype(jnp.float32)).astype(BF)
+        sn[near, 0, first, :] = (acc_near[held, 0, first, :] + rh[far, first, :].astype(jnp.float32)).astype(BF)
+        sn[near, 0, second, :] = acc_near[held, 0, second, :].astype(BF)
+        sn[near, 1, first, :] = acc_near[held, 1, first, :].astype(BF)
+        sn[near, 1, second, :] = (acc_near[held, 1, second, :] + rh[far, second, :].astype(jnp.float32)).astype(BF)
 
         @pl.when(u < units - FAR)
         def _():
@@ -544,7 +547,7 @@
             do(pltpu.make_async_copy(so.at[two, second], gu_hbm.at[layer, at, chunk_columns(chunk)], out_sem.at[two, 1]))
 
     def sum_all(u):
-        held, near, two = u % HELD, u % NEAR, u % 2
+        near, two = u % NEAR, u % 2
         arrived(rn.at[near, 0], rn_sem.at[near, 0])
         arrived(rn.at[near, 1], rn_sem.at[near, 1])
 
@@ -553,7 +556,7 @@
             arrived(so.at[two, first], out_sem.at[two, 0])
             arrived(so.at[two, second], out_sem.at[two, 1])
 
-        g = (acc[held, 0] + rn[near, 0].astype(jnp.float32) + rn[near, 1].astype(jnp.float32)).astype(BF)
+        g = (acc_own[u % (SUM_ALL + 1)] + rn[near, 0].astype(jnp.float32) + rn[near, 1].astype(jnp.float32)).astype(BF)
         so[two] = g
         wide_g = g.astype(jnp.float32)
         sq[...] += jnp.sum((wide_g * wide_g).reshape(2 * part // 8, 8, wide), axis=0)
@@ -645,8 +648,8 @@
     def tick(t, _):
         when_unit(t - SUM_ALL, sum_all)
         when_unit(t - SUM_NEAR, sum_near)
+        when_unit(t, compute)
         when_unit(t - SUM_CHIP, sum_chip)
-        when_unit(t, compute)
         return 0
 
     lax.fori_loop(0, units + SUM_ALL, tick, 0)
@@ -705,10 +708,12 @@
             vmem((tokens, d), jnp.float32),
             vmem((wide, d), BF),
             vmem((d, 2 * wide), BF),
-            vmem((2, 256, wide), jnp.float32),
-            vmem((2, 256, wide), jnp.float32),
+            vmem((2, 512, wide), jnp.float32),
+            vmem((2, 512, wide), jnp.float32),
             vmem((2, 256, d), BF),
-            vmem((HELD, n // 2, *block), jnp.float32),
+            vmem((SUM_CHIP + 1, *block), jnp.float32),
+            vmem((SUM_NEAR + 1, 2, *block), jnp.float32),
+            vmem((SUM_ALL + 1, *block), jnp.float32),
             vmem((2, n // 2, *block), BF),
             vmem((2, n // 2, *block), BF),
             vmem((FAR, *block), BF),

time: 729 us -> 624 us (0.86)
  Pallas kernels: 693 us -> 589 us
    pallas_call x1, Pallas kernels: 418 us -> 362 us  [backward(): pl.pallas_call(functools.partial(backward_kernel, n), out_shape=(shape((l...]
    pallas_call x1, Pallas kernels: 275 us -> 227 us  [forward(): pl.pallas_call(functools.partial(forward_kernel, n, wide, deep), out_shap...]
where the time goes in v2:
time: 624 us; the launch traced here: 623 us
  Pallas kernels  589 us (94%)
  other arithmetic  28.1 us (5%)
    pallas_call x1, Pallas kernels, backward(): pl.pallas_call(functools.partial(backward_kernel, n), out_shape=(shape((l...  362 us
    pallas_call x1, Pallas kernels, forward(): pl.pallas_call(functools.partial(forward_kernel, n, wide, deep), out_shap...  227 us
    convert_element_type x2, other arithmetic, adamw(): return ((w - 0.02 * step).astype(BF), m, v)  28.1 us

profile of v2, /device:TPU:113, one launch (start us, length us, event | category | flops | bytes accessed | tf_op | source)
XLA Modules:
  0.0 623.1 jit_solution(4116419180021905846)
XLA Ops:
  0.6 227.4 %shard_map.178 = (f32[2,2048,4480]{2,1,0:T(8,128)}, f32[2,2048,4480]{2,1,0:T(8,128)}, bf16[2,4480,2048]{2,1,0:T(8,128)(2,1)}, bf16[2,1280,2048]{2,1,0:T(8,128)(2...) custom-call(bf16[2048,1280]{1,0:T(8,128)(2,1)} %bitcast.3, ...), custom_call_target="tpu_custom_call" | custom-call | flops 117440512000 | bytes 293601280 | tf_op jit(solution)/shard_map/pallas_call | solution.py:293
  228.0 361.6 %shard_map.179 = (bf16[2,160,4480]{2,1,0:T(8,128)(2,1)}, bf16[2,160,4480]{2,1,0:T(8,128)(2,1)}, bf16[2,560,1280]{2,1,0:T(8,128)(2,1)}, f32[8,128]{1,0:T(8,128)}) custom-call(bf16[2048,1280]{1,0:T(8,128)(2,1)} %bitcast.4, bf16[2,2048,1280]{2,1,0:T(8,128)(2,1)} %get-tuple-element.21.h_hbm, bf16[2,1280,2048]{2,1,0:T(8,128)(2,1)} %get-tuple-element.22.at_hbm, ...), custom_call_target="tpu_custom_call" | custom-call | flops 234881024000 | bytes 293601280 | tf_op jit(solution)/shard_map/pallas_call | solution.py:695
  589.7 1.2 slice.3
  590.8 0.0 copy-start
  590.8 0.0 copy-start.1
  590.8 0.0 copy-start.2
  590.9 0.0 copy-start.3
  590.9 13.5 %fusion.8 = (bf16[2,560,1280]{2,1,0:T(8,128)(2,1)}, f32[2,560,1280]{2,1,0:T(8,128)}, f32[2,560,1280]{2,1,0:T(8,128)}) fusion(bf16[2,560,1280]{2,1,0:T(8,128)(2,1)} %wd_hbm.1, f32[]{:T(128)} %bitcast.2, bf16[2,560,1280]{2,1,0:T(8,128)(2,1)} %get-tuple-element.32, f32[2,560,1280]{2,1,0:T(8,128)} %param.21, f32[2,560,1280]{2,1,0:T(8,128)} %param.18), kind=kLoop, calls=%fused_computation.17 | loop fusion | flops 24371200 | bytes 31539204 | tf_op jit(solution)/shard_map/convert_element_type | solution.py:22
  604.4 0.0 copy-done
  604.4 0.5 copy-done.1
  604.8 2.0 copy-done.2
  606.9 1.6 copy-done.3
  608.5 14.6 %fusion.2 = (bf16[2,160,4480]{2,1,0:T(8,128)(2,1)}, f32[2,160,4480]{2,1,0:T(8,128)}, f32[2,160,4480]{2,1,0:T(8,128)}, bf16[2,160,4480]{2,1,0:T(8,128)(2,1)}, f32...) fusion(bf16[2,160,4480]{2,1,0:T(8,128)(2,1)} %wg_hbm.1, f32[]{:T(128)} %bitcast.2, ...), kind=kLoop, calls=%fused_computation.11 | loop fusion | flops 48742400 | bytes 63078404 | tf_op jit(solution)/shard_map/convert_element_type | solution.py:22
Async XLA Ops:
  590.8 13.5 %copy-start = (f32[2,160,4480]{2,1,0:T(8,128)S(1)}, f32[2,160,4480]{2,1,0:T(8,128)}, u32[]{:S(2)}) copy-start(f32[2,160,4480]{2,1,0:T(8,128)} %param.19) | copy-start | bytes 17203204
  590.8 14.0 %copy-start.1 = (f32[2,160,4480]{2,1,0:T(8,128)S(1)}, f32[2,160,4480]{2,1,0:T(8,128)}, u32[]{:S(2)}) copy-start(f32[2,160,4480]{2,1,0:T(8,128)} %param.16) | copy-start | bytes 17203204
  590.8 16.0 %copy-start.2 = (f32[2,160,4480]{2,1,0:T(8,128)S(1)}, f32[2,160,4480]{2,1,0:T(8,128)}, u32[]{:S(2)}) copy-start(f32[2,160,4480]{2,1,0:T(8,128)} %param.20) | copy-start | bytes 17203204
  590.9 17.6 %copy-start.3 = (f32[2,160,4480]{2,1,0:T(8,128)S(1)}, f32[2,160,4480]{2,1,0:T(8,128)}, u32[]{:S(2)}) copy-start(f32[2,160,4480]{2,1,0:T(8,128)} %param.17) | copy-start | bytes 17203204
